TPU v7x, 32 devices: a whole 2x2x4 slice. The times are simulated.
32 devices in a mesh: section: 8 (over z, y), tp: 4 (over x, core).
Axes of the slice: x: 2, y: 2, z: 4, core: 2. Of those that a mesh axis runs over, the one named last changes fastest.
Arguments:
- incoming: bfloat16 [8, 256, 6144], P('section', 'tp'), may hold values from -11 to 11, as said below
- grad_in: bfloat16 [8, 256, 6144], P('section', 'tp'), may hold values from -6 to 6
- held: bfloat16 [8, 2, 256, 6144], P('section', None, 'tp'), may hold values from -11 to 11, as said below
- roster: int32 [8, 2], replicated, may hold values from 0 to 1
- norm_gain: float32 [8, 6144], P('section'), may hold values from 0.25 to 1.75
- r_scores: float32 [8, 48, 256, 256], P('section', 'tp'), may hold values from -12 to 236
- value_weight: bfloat16 [8, 6144, 6144], P('section', None, 'tp'), may hold values from -0.078125 to 0.078125
- out_weight: bfloat16 [8, 6144, 6144], P('section', 'tp'), may hold values from -0.078125 to 0.078125
Outputs:
- act_out: bfloat16 [8, 256, 6144], P('section', 'tp')
- grad_out: bfloat16 [8, 256, 6144], P('section', 'tp')
- held_next: bfloat16 [8, 2, 256, 6144], P('section', None, 'tp')
Inputs may be any that keep to these rules, and one draw needn't show every extreme that they name: `incoming`: every token row has its own scale. `held`: every token row has its own scale. roster[s, 0] names the slot at section 7 - s that holds section s's stash to fetch; roster[s, 1] names the slot there that takes section s's evicted input; the two may be equal.
All inputs are finite; a program needn't handle non-finite values.
Results may differ from a plain program's by a relative error of at most 0.0036.
Values may be sent and summed in bfloat16 or wider, within the bound.
A program may use at most 128 MiB of HBM per device.

v0:
```python
import jax
import jax.numpy as jnp
from jax import lax
from jax.sharding import PartitionSpec as P

EPS = 0.5


def from_partner(value, axis, bit):
    return lax.ppermute(value, axis, [(i, i ^ 1 << bit) for i in range(lax.axis_size(axis))])


def from_behind(block, axis, distance):
    devices = range(lax.axis_size(axis))
    route = [((i - distance) % len(devices), i) for i in devices]
    return lax.ppermute(block, axis, route)


def row_scale(values):
    return jnp.sqrt(jnp.mean(values * values, axis=-1, keepdims=True) + EPS)


def causal_probs(scores):
    length = scores.shape[-1]
    query_pos = lax.broadcasted_iota(jnp.int32, (length, length), 0)
    key_pos = lax.broadcasted_iota(jnp.int32, (length, length), 1)
    allowed = key_pos <= query_pos
    masked = jnp.where(allowed, scores, -jnp.inf)
    highest = jnp.max(masked, axis=-1, keepdims=True)
    expo = jnp.where(allowed, jnp.exp(masked - highest), 0.0)
    return (expo / jnp.sum(expo, axis=-1, keepdims=True)).astype(jnp.bfloat16)


def body(incoming, grad_in, held, roster, norm_gain, r_scores, value_weight, out_weight):
    tokens_here = incoming[0]
    grad_here = grad_in[0]
    stash_store = held[0]
    gain = norm_gain[0]
    w_value = value_weight[0]
    w_out = out_weight[0]
    heads_here = r_scores.shape[1]
    seq_len = r_scores.shape[2]
    width = tokens_here.shape[1]
    attn_probs = causal_probs(r_scores[0])
    sections = lax.axis_size("section")
    mirror = sections - 1 - lax.axis_index("section")
    mirror_plan = lax.dynamic_index_in_dim(roster, mirror, 0, keepdims=False)
    outgoing = lax.dynamic_index_in_dim(stash_store, mirror_plan[0], 0, keepdims=False)
    bit_count = sections.bit_length() - 1
    bit_order = list(range(bit_count))
    travelling = (tokens_here, outgoing)
    for which_bit in bit_order:
        travelling = from_partner((travelling[0], travelling[1]), "section", which_bit)
    arriving, fetched = travelling
    slot_match = jnp.arange(stash_store.shape[0]) == mirror_plan[1]
    held_next = jnp.where(slot_match[:, None, None], arriving[None], stash_store)
    tokens_f32 = tokens_here.astype(jnp.float32)
    normed = (tokens_f32 / row_scale(tokens_f32) * gain).astype(jnp.bfloat16)
    values = jnp.dot(
        lax.all_gather(normed, "tp", axis=0, tiled=True),
        w_value,
        preferred_element_type=jnp.float32,
    ).astype(jnp.bfloat16)
    context = jnp.einsum(
        "hij,jhd->ihd",
        attn_probs,
        values.reshape(seq_len, heads_here, -1),
        preferred_element_type=jnp.float32,
    )
    context = context.astype(jnp.bfloat16).reshape(seq_len, -1)
    block = context
    update = lax.psum_scatter(
        jnp.dot(block, w_out, preferred_element_type=jnp.float32),
        "tp",
        scatter_dimension=0,
        tiled=True,
    )
    layer_out = (tokens_f32 + update).astype(jnp.bfloat16)
    passed_on = from_behind(layer_out, "section", 1)
    grad_context = lax.dot_general(
        lax.all_gather(grad_here, "tp", axis=0, tiled=True),
        w_out,
        (((1,), (1,)), ((), ())),
        preferred_element_type=jnp.float32,
    ).astype(jnp.bfloat16)
    grad_values = jnp.einsum(
        "hij,ihd->jhd",
        attn_probs,
        grad_context.reshape(seq_len, heads_here, -1),
        preferred_element_type=jnp.float32,
    )
    grad_values = grad_values.astype(jnp.bfloat16).reshape(seq_len, -1)
    block = grad_values
    grad_normed = lax.psum_scatter(
        lax.dot_general(
            block, w_value, (((1,), (1,)), ((), ())), preferred_element_type=jnp.float32
        ),
        "tp",
        scatter_dimension=0,
        tiled=True,
    )
    stash_f32 = fetched.astype(jnp.float32)
    stash_scale = row_scale(stash_f32)
    inner_sum = jnp.sum(gain * grad_normed * stash_f32, axis=-1, keepdims=True)
    input_grad = (
        grad_here.astype(jnp.float32)
        + gain * grad_normed / stash_scale
        - stash_f32 * inner_sum / (width * stash_scale**3)
    )
    returned = from_behind(input_grad.astype(jnp.bfloat16), "section", -1)
    return (passed_on[None], returned[None], held_next[None])


def solution(mesh):
    in_specs = (
        P("section", "tp", None),
        P("section", "tp", None),
        P("section", None, "tp", None),
        P(),
        P("section", None),
        P("section", "tp", None, None),
        P("section", None, "tp"),
        P("section", "tp", None),
    )
    out_specs = (P("section", "tp", None), P("section", "tp", None), P("section", None, "tp", None))
    return jax.shard_map(body, mesh=mesh, in_specs=in_specs, out_specs=out_specs, check_vma=False)
```

profile of v0, /device:TPU:12, one launch (start us, length us, event | category | flops | bytes accessed | tf_op | source)
XLA Modules:
  0.0 306.1 jit_solution(16464106507098621147)
XLA Ops:
  7.2 0.0 all-gather.6.cloned.1.call-start
  7.2 0.7 all-gather.6.cloned.1.call-update
  7.9 0.0 reduce-scatter.5.cloned.1.call-start
  8.0 4.4 %fusion.33 = (f32[12,256]{1,0:T(8,128)S(1)}, f32[12,256,256]{2,1,0:T(8,128)S(1)}) fusion(f32[1,12,256,256]{3,2,1,0:T(8,128)} %param.13, pred[256,256]{1,0:T(8,128)(4,1)S(1)} %iota_compare_fusion), kind=kOutput, calls=%fused_computation.47 | output fusion | flops 3932415 | bytes 6369280 | tf_op jit(solution)/shard_map/sub | solution.py:30
  12.4 0.5 divide_convert_fusion
  12.9 26.3 %all-gather.6.cloned.1.call-done = bf16[1,256,6144]{2,1,0:T(8,128)(2,1)} async-done(((bf16[1,64,6144]{2,1,0:T(8,128)(2,1)}), bf16[1,256,6144]{2,1,0:T(8,128)(2,1)}) %all-gather.6.cloned.1.call-update) | async-done | bytes 3145744 | tf_op jit(solution)/shard_map/all_gather | solution.py:81
  39.2 9.9 %fusion.14 = bf16[256,1536]{1,0:T(8,128)(2,1)S(1)} fusion(bf16[1,1536,6144]{2,1,0:T(8,128)(2,1)} %param.15, bf16[1,256,6144]{2,1,0:T(8,128)(2,1)} %all-gather.6.cloned.1.call-done), kind=kOutput, calls=%fused_computation.15 | convolution fusion | flops 4832231424 | bytes 22806528 | tf_op jit(solution)/shard_map/dot_general | solution.py:80
  49.1 0.3 copy.14
  49.4 0.4 convolution_convert_fusion
  49.8 11.7 %fusion.5 = f32[256,6144]{1,0:T(8,128)} fusion(bf16[256,1536]{0,1:T(8,128)(2,1)S(1)} %bitcast.64, bf16[1,6144,1536]{2,1,0:T(8,128)(2,1)} %param.14), kind=kOutput, calls=%fused_computation.5 | convolution fusion | flops 4831838208 | bytes 25952256 | tf_op jit(solution)/shard_map/dot_general | solution.py:95
  61.5 0.0 reduce-scatter.5.cloned.1.call-update
  61.5 0.0 all-gather.4.cloned.1.call-start
  61.6 0.1 constant_dynamic-slice_fusion
  61.7 0.5 fusion.32
  64.1 1.2 dynamic-slice_bitcast_fusion
  65.3 0.6 collective-permute-start.1
  66.0 19.1 %collective-permute-done.1 = bf16[64,6144]{1,0:T(8,128)(2,1)S(1)} collective-permute-done((bf16[64,6144]{1,0:T(8,128)(2,1)S(1)}, bf16[64,6144]{1,0:T(8,128)(2,1)S(1)}, u32[]{:S(2)}, u32[]{:S(2)}) %collective-permute-start.1) | collective-permute-done | bytes 786464 | tf_op jit(solution)/shard_map/ppermute | solution.py:10
  85.1 0.5 collective-permute-start.2
  85.6 18.3 %collective-permute-done.2 = bf16[64,6144]{1,0:T(8,128)(2,1)S(1)} collective-permute-done((bf16[64,6144]{1,0:T(8,128)(2,1)S(1)}, bf16[64,6144]{1,0:T(8,128)(2,1)S(1)}, u32[]{:S(2)}, u32[]{:S(2)}) %collective-permute-start.2) | collective-permute-done | bytes 786464 | tf_op jit(solution)/shard_map/ppermute | solution.py:10
  103.9 2.4 collective-permute-start.3
  106.3 0.3 fusion.19
  106.6 32.2 %collective-permute-done.3 = bf16[64,6144]{1,0:T(8,128)(2,1)} collective-permute-done((bf16[64,6144]{1,0:T(8,128)(2,1)S(1)}, bf16[64,6144]{1,0:T(8,128)(2,1)}, u32[]{:S(2)}, u32[]{:S(2)}) %collective-permute-start.3) | collective-permute-done | bytes 786464 | tf_op jit(solution)/shard_map/ppermute | solution.py:10
  138.8 2.2 fusion.24
  141.0 3.1 %fusion.27 = (bf16[64,6144]{1,0:T(8,128)(2,1)}, bf16[64,6144]{1,0:T(8,128)(2,1)}) fusion(bf16[64,6144]{1,0:T(8,128)(2,1)} %collective-permute-done.3, f32[64,6144]{1,0:T(8,128)S(1)} %copy-done.3, bf16[1,64,6144]{2,1,0:T(8,128)(2,1)S(1)} %copy-done.5, f32[64]{0:T(128)S(1)} %get-tuple-element.10, f32[64]{0:T(128)S(1)} %get-tuple-element.3, ...), kind=kLoop, calls=%fused_computation.30 | loop fusion | flops 5111808 | bytes 5530624 | tf_op jit(solution)/shard_map/convert_element_type | solution.py:110
  144.0 0.0 all-gather.4.cloned.1.call-update
  144.1 0.2 reduce-scatter.3.cloned.1.call-start
  144.3 29.5 %all-gather.4.cloned.1.call-done = bf16[256,6144]{1,0:T(8,128)(2,1)} async-done(((bf16[64,6144]{1,0:T(8,128)(2,1)}), bf16[256,6144]{1,0:T(8,128)(2,1)}) %all-gather.4.cloned.1.call-update) | async-done | bytes 3145744 | tf_op jit(solution)/shard_map/all_gather | solution.py:60
  173.8 10.6 %fusion.11 = bf16[256,1536]{1,0:T(8,128)(2,1)} fusion(bf16[256,6144]{1,0:T(8,128)(2,1)} %all-gather.4.cloned.1.call-done, bf16[1,6144,1536]{2,1,0:T(8,128)(2,1)} %param.14), kind=kOutput, calls=%fused_computation.14 | convolution fusion | flops 4832231424 | bytes 22806528 | tf_op jit(solution)/shard_map/dot_general | solution.py:59
  184.4 1.4 copy.13
  185.8 0.6 convolution_convert_fusion.1
  186.5 13.6 %fusion.3 = f32[256,6144]{1,0:T(8,128)} fusion(bf16[256,1536]{0,1:T(8,128)(2,1)S(1)} %bitcast.60, bf16[1,1536,6144]{2,1,0:T(8,128)(2,1)} %param.15), kind=kOutput, calls=%fused_computation.3 | convolution fusion | flops 4831838208 | bytes 25952256 | tf_op jit(solution)/shard_map/dot_general | solution.py:73
  200.0 0.0 reduce-scatter.3.cloned.1.call-update
  200.1 0.6 collective-permute-start.5
  200.7 19.1 %collective-permute-done.5 = bf16[64,6144]{1,0:T(8,128)(2,1)S(1)} collective-permute-done((bf16[64,6144]{1,0:T(8,128)(2,1)S(1)}, bf16[64,6144]{1,0:T(8,128)(2,1)S(1)}, u32[]{:S(2)}, u32[]{:S(2)}) %collective-permute-start.5) | collective-permute-done | bytes 786464 | tf_op jit(solution)/shard_map/ppermute | solution.py:10
  219.8 0.5 collective-permute-start.6
  220.3 0.6 iota_compare_fusion.1
  221.0 17.7 %collective-permute-done.6 = bf16[64,6144]{1,0:T(8,128)(2,1)} collective-permute-done((bf16[64,6144]{1,0:T(8,128)(2,1)S(1)}, bf16[64,6144]{1,0:T(8,128)(2,1)}, u32[]{:S(2)}, u32[]{:S(2)}) %collective-permute-start.6) | collective-permute-done | bytes 786464 | tf_op jit(solution)/shard_map/ppermute | solution.py:10
  238.7 2.4 collective-permute-start.7
  241.1 0.6 collective-permute-start.4
  241.7 17.4 %reduce-scatter.3.cloned.1.call-done = f32[64,6144]{1,0:T(8,128)} async-done(((f32[256,6144]{1,0:T(8,128)}), f32[64,6144]{1,0:T(8,128)}) %reduce-scatter.3.cloned.1.call-update) | async-done | bytes 1572880 | tf_op jit(solution)/shard_map/reduce_scatter | solution.py:72
  259.0 1.6 fusion.22
  260.6 1.5 collective-permute-start
  262.2 11.7 %collective-permute-done.7 = bf16[64,6144]{1,0:T(8,128)(2,1)} collective-permute-done((bf16[64,6144]{1,0:T(8,128)(2,1)}, bf16[64,6144]{1,0:T(8,128)(2,1)}, u32[]{:S(2)}, u32[]{:S(2)}) %collective-permute-start.7) | collective-permute-done | bytes 786464 | tf_op jit(solution)/shard_map/ppermute | solution.py:10
  273.9 2.6 broadcast_select_fusion
  276.5 14.3 %collective-permute-done.4 = bf16[64,6144]{1,0:T(8,128)(2,1)} collective-permute-done((bf16[64,6144]{1,0:T(8,128)(2,1)S(1)}, bf16[64,6144]{1,0:T(8,128)(2,1)}, u32[]{:S(2)}, u32[]{:S(2)}) %collective-permute-start.4) | collective-permute-done | bytes 786464 | tf_op jit(solution)/shard_map/ppermute | solution.py:16
  290.8 5.9 %collective-permute-done = bf16[64,6144]{1,0:T(8,128)(2,1)S(1)} collective-permute-done((bf16[64,6144]{1,0:T(8,128)(2,1)S(1)}, bf16[64,6144]{1,0:T(8,128)(2,1)S(1)}, u32[]{:S(2)}, u32[]{:S(2)}) %collective-permute-start) | collective-permute-done | bytes 786464 | tf_op jit(solution)/shard_map/ppermute | solution.py:16
  296.7 0.9 copy.17
  297.5 2.1 copy.18
  (20 shorter events, 0.1 us)
Async XLA Ops:
  7.2 54.4 %copy-start = (s32[8,2]{0,1:T(2,128)S(1)}, s32[8,2]{0,1:T(2,128)}, u32[]{:S(2)}) copy-start(s32[8,2]{0,1:T(2,128)} %param.11) | copy-start | bytes 196
  7.2 32.0 %all-gather.6.cloned.1.call-start = ((), (), s32[]{:S(2)}) async-start(), calls=%async_computation.5 | async-start | bytes 3932160 | tf_op jit(solution)/shard_map/all_gather | solution.py:81
  7.9 130.8 %reduce-scatter.5.cloned.1.call-start = ((), (), s32[]{:S(2)}) async-start(), calls=%async_computation.4 | async-start | bytes 7864320 | tf_op jit(solution)/shard_map/reduce_scatter | solution.py:94
  61.5 44.8 %copy-start.2 = (bf16[1,64,6144]{2,1,0:T(8,128)(2,1)S(1)}, bf16[1,64,6144]{2,1,0:T(8,128)(2,1)}, u32[]{:S(2)}) copy-start(bf16[1,64,6144]{2,1,0:T(8,128)(2,1)} %param.8) | copy-start | bytes 2359300
  61.5 77.2 %copy-start.7 = (f32[1,6144]{1,0:T(1,128)S(1)}, f32[1,6144]{1,0:T(1,128)}, u32[]{:S(2)}) copy-start(f32[1,6144]{1,0:T(1,128)} %param.12) | copy-start | bytes 73732
  61.5 112.3 %all-gather.4.cloned.1.call-start = ((), (), s32[]{:S(2)}) async-start(), calls=%async_computation.2 | async-start | bytes 3932160 | tf_op jit(solution)/shard_map/all_gather | solution.py:60
  65.3 75.6 %copy-start.5 = (bf16[1,64,6144]{2,1,0:T(8,128)(2,1)S(1)}, bf16[1,64,6144]{2,1,0:T(8,128)(2,1)}, u32[]{:S(2)}) copy-start(bf16[1,64,6144]{2,1,0:T(8,128)(2,1)} %param.9) | copy-start | bytes 2359300
  65.3 19.8 %collective-permute-start.1 = (bf16[64,6144]{1,0:T(8,128)(2,1)S(1)}, bf16[64,6144]{1,0:T(8,128)(2,1)S(1)}, u32[]{:S(2)}, u32[]{:S(2)}) collective-permute-start(bf16[64,6144]{1,0:T(8,128)(2,1)S(1)} %dynamic-slice_bitcast_fusion), channel_id=1, source_target_pairs={{0,4},{4,0},{8,12},{12,8},{16,20},{20,16},{24,28},{28,24},{1,5},{5... | collective-permute-start | bytes 2359304 | tf_op jit(solution)/shard_map/ppermute | solution.py:10
  85.1 18.8 %collective-permute-start.2 = (bf16[64,6144]{1,0:T(8,128)(2,1)S(1)}, bf16[64,6144]{1,0:T(8,128)(2,1)S(1)}, u32[]{:S(2)}, u32[]{:S(2)}) collective-permute-start(bf16[64,6144]{1,0:T(8,128)(2,1)S(1)} %collective-permute-done.1), channel_id=1, source_target_pairs={{0,8},{4,12},{8,0},{12,4},{16,24},{20,28},{24,16},{28,20},{1,9},{5... | collective-permute-start | bytes 2359304 | tf_op jit(solution)/shard_map/ppermute | solution.py:10
  103.9 34.8 %collective-permute-start.3 = (bf16[64,6144]{1,0:T(8,128)(2,1)S(1)}, bf16[64,6144]{1,0:T(8,128)(2,1)}, u32[]{:S(2)}, u32[]{:S(2)}) collective-permute-start(bf16[64,6144]{1,0:T(8,128)(2,1)S(1)} %collective-permute-done.2), channel_id=1, source_target_pairs={{0,16},{4,20},{8,24},{12,28},{16,0},{20,4},{24,8},{28,12},{1,17},{... | collective-permute-start | bytes 2359304 | tf_op jit(solution)/shard_map/ppermute | solution.py:10
  138.8 2.2 copy-start.3
  144.1 115.0 %reduce-scatter.3.cloned.1.call-start = ((), (), s32[]{:S(2)}) async-start(), calls=%async_computation.3 | async-start | bytes 7864320 | tf_op jit(solution)/shard_map/reduce_scatter | solution.py:72
  200.0 41.1 %copy-start.6 = (bf16[64,6144]{1,0:T(8,128)(2,1)S(1)}, bf16[64,6144]{1,0:T(8,128)(2,1)}, u32[]{:S(2)}) copy-start(bf16[64,6144]{1,0:T(8,128)(2,1)} %get-tuple-element.5) | copy-start | bytes 2359300
  200.1 19.7 %collective-permute-start.5 = (bf16[64,6144]{1,0:T(8,128)(2,1)S(1)}, bf16[64,6144]{1,0:T(8,128)(2,1)S(1)}, u32[]{:S(2)}, u32[]{:S(2)}) collective-permute-start(bf16[64,6144]{1,0:T(8,128)(2,1)S(1)} %bitcast.59), channel_id=1, source_target_pairs={{0,4},{4,0},{8,12},{12,8},{16,20},{20,16},{24,28},{28,24},{1,5},{5... | collective-permute-start | bytes 2359304 | tf_op jit(solution)/shard_map/ppermute | solution.py:10
  219.8 18.9 %collective-permute-start.6 = (bf16[64,6144]{1,0:T(8,128)(2,1)S(1)}, bf16[64,6144]{1,0:T(8,128)(2,1)}, u32[]{:S(2)}, u32[]{:S(2)}) collective-permute-start(bf16[64,6144]{1,0:T(8,128)(2,1)S(1)} %collective-permute-done.5), channel_id=1, source_target_pairs={{0,8},{4,12},{8,0},{12,4},{16,24},{20,28},{24,16},{28,20},{1,9},{5... | collective-permute-start | bytes 2359304 | tf_op jit(solution)/shard_map/ppermute | solution.py:10
  238.7 35.2 %collective-permute-start.7 = (bf16[64,6144]{1,0:T(8,128)(2,1)}, bf16[64,6144]{1,0:T(8,128)(2,1)}, u32[]{:S(2)}, u32[]{:S(2)}) collective-permute-start(bf16[64,6144]{1,0:T(8,128)(2,1)} %collective-permute-done.6), channel_id=1, source_target_pairs={{0,16},{4,20},{8,24},{12,28},{16,0},{20,4},{24,8},{28,12},{1,17},{... | collective-permute-start | bytes 2359304 | tf_op jit(solution)/shard_map/ppermute | solution.py:10
  241.1 32.8 %copy-start.4 = (bf16[1,2,64,6144]{3,2,1,0:T(8,128)(2,1)S(1)}, bf16[1,2,64,6144]{3,2,1,0:T(8,128)(2,1)}, u32[]{:S(2)}) copy-start(bf16[1,2,64,6144]{3,2,1,0:T(8,128)(2,1)} %param.10) | copy-start | bytes 4718596
  241.1 49.7 %collective-permute-start.4 = (bf16[64,6144]{1,0:T(8,128)(2,1)S(1)}, bf16[64,6144]{1,0:T(8,128)(2,1)}, u32[]{:S(2)}, u32[]{:S(2)}) collective-permute-start(bf16[64,6144]{1,0:T(8,128)(2,1)S(1)} %copy-done.6), channel_id=1, source_target_pairs={{4,0},{8,4},{12,8},{16,12},{20,16},{24,20},{28,24},{0,28},{5,1},{9... | collective-permute-start | bytes 2359304 | tf_op jit(solution)/shard_map/ppermute | solution.py:16
  260.6 36.0 %collective-permute-start = (bf16[64,6144]{1,0:T(8,128)(2,1)S(1)}, bf16[64,6144]{1,0:T(8,128)(2,1)S(1)}, u32[]{:S(2)}, u32[]{:S(2)}) collective-permute-start(bf16[64,6144]{1,0:T(8,128)(2,1)S(1)} %fusion.22), channel_id=1, source_target_pairs={{28,0},{0,4},{4,8},{8,12},{12,16},{16,20},{20,24},{24,28},{29,1},{... | collective-permute-start | bytes 2359304 | tf_op jit(solution)/shard_map/ppermute | solution.py:16
  296.7 2.9 copy-start.1
Sparse Core Ops, SparseCore 0:
  9.5 29.6 all-gather.5
  61.6 58.8 reduce-scatter.4
  144.2 29.5 all-gather.3
  200.2 58.8 reduce-scatter.2
where the time goes:
time: 307 us; the launch traced here: 306 us
  waiting for transfers between devices  212 us (69%)
  matrix products  46.8 us (15%)
  between operations  15.9 us (5%)
  other arithmetic  15.2 us (5%)
  starting transfers between devices  9.55 us (3%)
  local copies, waits for them, and re-layouts  6.44 us (2%)
    ppermute x6, waiting for transfers between devices, from_partner(): lax.ppermute(value, axis, [(i, i ^ 1 << bit) for i in range(lax.axis_size...  118 us
    all_gather x1, waiting for transfers between devices, body(): lax.all_gather(normed, 'tp', axis=0, tiled=True)  29.5 us
    all_gather x1, waiting for transfers between devices, body(): lax.all_gather(grad_here, 'tp', axis=0, tiled=True)  26.3 us
    ppermute x2, waiting for transfers between devices, from_behind(): return lax.ppermute(block, axis, route)  20.2 us
    reduce_scatter x1, waiting for transfers between devices, body(): lax.psum_scatter(jnp.dot(block, w_out, preferred_element_type=jnp.float32...  17.4 us
    dot_general x1, matrix products, body(): jnp.dot(block, w_out, preferred_element_type=jnp.float32)  13.6 us
    dot_general x1, matrix products, body(): lax.dot_general(block, w_value, (((1,), (1,)), ((), ())), preferred_eleme...  11.7 us
    dot_general x1, matrix products, body(): jnp.dot(lax.all_gather(normed, 'tp', axis=0, tiled=True), w_value, prefer...  10.6 us
  transfers between devices with their start and end apart: 12, of which 11 were waited for; matrix products, arithmetic and copies ran while one was open for 4% of the time, Pallas kernels for 0%

commit v1 on v0

v1 whole, which is shorter than its diff:
```python
import jax
import jax.numpy as jnp
from jax import lax
from jax.sharding import PartitionSpec as P


EPS = 0.5


CHUNKS = 2


def from_partner(value, bit):
    return lax.ppermute(value, "tp", [(i, i ^ 1 << bit) for i in range(lax.axis_size("tp"))])


def from_behind(block, distance):
    devices = range(lax.axis_size("section"))
    return lax.ppermute(block, "section", [((i - distance) % len(devices), i) for i in devices])


def from_mirror(block):
    devices = range(lax.axis_size("section"))
    return lax.ppermute(block, "section", [(len(devices) - 1 - i, i) for i in devices])


def tp_bits():
    return lax.axis_size("tp").bit_length() - 1


def own_bit(bit):
    return lax.axis_index("tp") >> bit & 1


def gather_rows(block):
    blocks = block
    for done, bit in enumerate(reversed(range(tp_bits()))):
        other = from_partner(blocks, bit)
        first = own_bit(bit) == 0
        blocks = jnp.stack(
            [jnp.where(first, blocks, other), jnp.where(first, other, blocks)], axis=done
        )
    return blocks.reshape(-1, block.shape[1])


def scatter_rows(partial):
    bits = tp_bits()
    part = partial.reshape((2,) * bits + (-1, partial.shape[1]))
    for bit in range(bits):
        at = bits - 1 - bit
        keep = lax.dynamic_index_in_dim(part, own_bit(bit), at, keepdims=False)
        give = lax.dynamic_index_in_dim(part, 1 - own_bit(bit), at, keepdims=False)
        got = from_partner(give.astype(jnp.bfloat16), bit)
        part = keep.astype(jnp.float32) + got.astype(jnp.float32)
    return part


def row_scale(values):
    return jnp.sqrt(jnp.mean(values * values, axis=-1, keepdims=True) + EPS)


def causal_probs(scores):
    length = scores.shape[-1]
    query_pos = lax.broadcasted_iota(jnp.int32, (length, length), 0)
    key_pos = lax.broadcasted_iota(jnp.int32, (length, length), 1)
    allowed = key_pos <= query_pos
    masked = jnp.where(allowed, scores, -jnp.inf)
    highest = jnp.max(masked, axis=-1, keepdims=True)
    expo = jnp.where(allowed, jnp.exp(masked - highest), 0.0)
    return (expo / jnp.sum(expo, axis=-1, keepdims=True)).astype(jnp.bfloat16)


def body(incoming, grad_in, held, roster, norm_gain, r_scores, value_weight, out_weight):
    tokens_here = incoming[0]
    grad_here = grad_in[0]
    stash_store = held[0]
    gain = norm_gain[0]
    w_value = value_weight[0]
    w_out = out_weight[0]
    heads_here = r_scores.shape[1]
    seq_len = r_scores.shape[2]
    width = tokens_here.shape[1]
    sections = lax.axis_size("section")
    mirror = sections - 1 - lax.axis_index("section")
    mirror_plan = lax.dynamic_index_in_dim(roster, mirror, 0, keepdims=False)

    tokens_f32 = tokens_here.astype(jnp.float32)
    normed = (tokens_f32 / row_scale(tokens_f32) * gain).astype(jnp.bfloat16)
    outgoing = lax.dynamic_index_in_dim(stash_store, mirror_plan[0], 0, keepdims=False)
    fetched = from_mirror(outgoing)
    arriving = from_mirror(tokens_here)
    all_grads = gather_rows(grad_here)
    all_normed = gather_rows(normed)
    fetched, _ = lax.optimization_barrier((fetched, all_normed))
    attn_probs = causal_probs(r_scores[0])

    grad_context = lax.dot_general(
        all_grads, w_out, (((1,), (1,)), ((), ())), preferred_element_type=jnp.float32
    ).astype(jnp.bfloat16)
    grad_values = jnp.einsum(
        "hij,ihd->jhd",
        attn_probs,
        grad_context.reshape(seq_len, heads_here, -1),
        preferred_element_type=jnp.float32,
    )
    grad_values = grad_values.astype(jnp.bfloat16).reshape(seq_len, -1)
    grad_normed = scatter_rows(
        lax.dot_general(
            grad_values, w_value, (((1,), (1,)), ((), ())), preferred_element_type=jnp.float32
        ),
    )
    stash_f32 = fetched.astype(jnp.float32)
    stash_scale = row_scale(stash_f32)
    inner_sum = jnp.sum(gain * grad_normed * stash_f32, axis=-1, keepdims=True)
    input_grad = (
        grad_here.astype(jnp.float32)
        + gain * grad_normed / stash_scale
        - stash_f32 * inner_sum / (width * stash_scale**3)
    )
    returned = from_behind(input_grad.astype(jnp.bfloat16), -1)

    values = jnp.dot(all_normed, w_value, preferred_element_type=jnp.float32)
    values = values.astype(jnp.bfloat16)
    context = jnp.einsum(
        "hij,jhd->ihd",
        attn_probs,
        values.reshape(seq_len, heads_here, -1),
        preferred_element_type=jnp.float32,
    )
    context = context.astype(jnp.bfloat16).reshape(seq_len, -1)
    passed_on = []
    span = width // CHUNKS
    for k in range(CHUNKS):
        columns = slice(k * span, (k + 1) * span)
        share = jnp.dot(context, w_out[:, columns], preferred_element_type=jnp.float32)
        update = scatter_rows(share)
        residual = tokens_here[:, columns]
        if k > 0:
            residual, layer_out = lax.optimization_barrier((residual, layer_out))
        layer_out = (residual.astype(jnp.float32) + update).astype(jnp.bfloat16)
        passed_on.append(from_behind(layer_out, 1))
    passed_on = jnp.concatenate(passed_on, axis=1)
    slot_match = jnp.arange(stash_store.shape[0]) == mirror_plan[1]
    held_next = jnp.where(slot_match[:, None, None], arriving[None], stash_store)
    return (passed_on[None], returned[None], held_next[None])


def solution(mesh):
    in_specs = (
        P("section", "tp", None),
        P("section", "tp", None),
        P("section", None, "tp", None),
        P(),
        P("section", None),
        P("section", "tp", None, None),
        P("section", None, "tp"),
        P("section", "tp", None),
    )
    out_specs = (P("section", "tp", None), P("section", "tp", None), P("section", None, "tp", None))
    return jax.shard_map(body, mesh=mesh, in_specs=in_specs, out_specs=out_specs, check_vma=False)
```

time: 307 us -> 170 us (0.55)
  waiting for transfers between devices: 212 us -> 63.9 us
  between operations: 15.9 us -> 3.05 us
  local copies, waits for them, and re-layouts: 6.44 us -> 17.7 us
  other arithmetic: 15.2 us -> 23.8 us
  starting transfers between devices: 9.55 us -> 13.3 us
    ppermute x8 -> x15, waiting for transfers between devices: 138 us -> 63.9 us  [the longest x10 48.2 us: from_partner(): lax.ppermute(value, 'tp', [(i, i ^ 1 << bit) for i in range(lax.axis_size...]
    all_gather x2 -> x0, waiting for transfers between devices: 55.9 us -> none  [the longest x1 29.5 us: body(): lax.all_gather(normed, 'tp', axis=0, tiled=True)]
    reduce_scatter x2 -> x0, waiting for transfers between devices: 17.4 us -> none  [the longest x1 17.4 us: body(): lax.psum_scatter(jnp.dot(block, w_out, preferred_element_type=jnp.float32...]
    another operation x0 -> x8, other arithmetic: none -> 7.28 us  [gather_rows(): jnp.stack([jnp.where(first, blocks, other), jnp.where(first, other, block...]
    convert_element_type x2 -> x10, local copies, waits for them, and re-layouts: 1.67 us -> 7.65 us  [the longest x1 2.61 us: body(): context = context.astype(jnp.bfloat16).reshape(seq_len, -1)]
    dot_general x4 -> x5, matrix products: 45.8 us -> 40.8 us  [the longest x2 16.4 us: body(): jnp.dot(context, w_out[:, columns], preferred_element_type=jnp.float32)]
    ppermute x8 -> x15, starting transfers between devices: 9.21 us -> 13.3 us  [the longest x10 6.65 us: from_partner(): lax.ppermute(value, 'tp', [(i, i ^ 1 << bit) for i in range(lax.axis_size...]
  transfers between devices with their start and end apart: 12 -> 15, of which waited for: 11 -> 7; matrix products, arithmetic and copies ran while one was open for 4% -> 49% of each run, Pallas kernels for 0% -> 0%
where the time goes in v1:
time: 170 us; the launch traced here: 167 us
  waiting for transfers between devices  63.9 us (38%)
  matrix products  45 us (26%)
  other arithmetic  23.8 us (14%)
  local copies, waits for them, and re-layouts  17.7 us (10%)
  starting transfers between devices  13.3 us (8%)
  between operations  3.05 us (2%)
    ppermute x10, waiting for transfers between devices, from_partner(): lax.ppermute(value, 'tp', [(i, i ^ 1 << bit) for i in range(lax.axis_size...  48.2 us
    dot_general x2, matrix products, body(): jnp.dot(context, w_out[:, columns], preferred_element_type=jnp.float32)  16.4 us
    ppermute x3, waiting for transfers between devices, from_behind(): lax.ppermute(block, 'section', [((i - distance) % len(devices), i) for i...  15.7 us
    dot_general x1, matrix products, body(): lax.dot_general(grad_values, w_value, (((1,), (1,)), ((), ())), preferred...  9.39 us
    dot_general x1, matrix products, body(): lax.dot_general(all_grads, w_out, (((1,), (1,)), ((), ())), preferred_ele...  9.1 us
    another operation x8, other arithmetic, gather_rows(): jnp.stack([jnp.where(first, blocks, other), jnp.where(first, other, block...  7.28 us
    ppermute x10, starting transfers between devices, from_partner(): lax.ppermute(value, 'tp', [(i, i ^ 1 << bit) for i in range(lax.axis_size...  6.65 us
    dot_general x1, matrix products, body(): values = jnp.dot(all_normed, w_value, preferred_element_type=jnp.float32)  5.9 us
  transfers between devices with their start and end apart: 15, of which 7 were waited for; matrix products, arithmetic and copies ran while one was open for 49% of the time, Pallas kernels for 0%

profile of v1, /device:TPU:12, one launch (start us, length us, event | category | flops | bytes accessed | tf_op | source)
XLA Modules:
  0.0 166.8 jit_solution(8530333464295100383)
XLA Ops:
  0.7 1.6 collective-permute-start.8
  2.2 1.4 fusion.11
  3.6 1.5 fusion.13
  5.1 0.6 collective-permute-start
  8.3 1.0 dynamic-slice_bitcast_fusion
  9.2 1.5 collective-permute-start.12
  10.8 1.4 collective-permute-start.14
  12.2 0.7 iota_compare_fusion.1
  12.9 4.5 %fusion.38 = (f32[12,256]{1,0:T(8,128)S(1)}, f32[12,256,256]{2,1,0:T(8,128)S(1)}) fusion(f32[1,12,256,256]{3,2,1,0:T(8,128)} %param.13, pred[256,256]{1,0:T(8,128)(4,1)S(1)} %iota_compare_fusion), kind=kOutput, calls=%fused_computation.82 | output fusion | flops 3932415 | bytes 6369280 | tf_op jit(solution)/shard_map/sub | solution.py:69
  17.9 19.2 %collective-permute-done = bf16[64,6144]{1,0:T(8,128)(2,1)} collective-permute-done((bf16[64,6144]{1,0:T(8,128)(2,1)S(1)}, bf16[64,6144]{1,0:T(8,128)(2,1)}, u32[]{:S(2)}, u32[]{:S(2)}) %collective-permute-start) | collective-permute-done | bytes 786464 | tf_op jit(solution)/shard_map/ppermute | solution.py:14
  37.2 1.6 select_bitcast_fusion.7
  39.1 0.9 copy-done.7
  40.0 1.6 select_bitcast_fusion.5
  41.6 1.4 pad_maximum_fusion.3
  43.9 1.3 slice-done.3
  45.2 0.7 slice-done.4
  45.9 5.9 %fusion.8 = bf16[256,1536]{1,0:T(8,128)(2,1)} fusion(bf16[256,6144]{1,0:T(8,128)(2,1)S(1)} %bitcast.134, bf16[1,6144,1536]{2,1,0:T(8,128)(2,1)S(1)} %bitcast.147), kind=kOutput, calls=%fused_computation.18 | convolution fusion | flops 4832231424 | bytes 22806528 | tf_op jit(solution)/shard_map/dot_general | solution.py:122
  51.8 2.3 %copy.19 = bf16[256,1536]{0,1:T(8,128)(2,1)} copy(bf16[256,1536]{1,0:T(8,128)(2,1)} %fusion.8) | data formatting | bytes 1572864 | tf_op jit(solution)/shard_map/convert_element_type | solution.py:123
  54.1 2.7 %fusion.23 = bf16[256,12,128]{0,2,1:T(8,128)(2,1)} fusion(bf16[256,12,128]{0,2,1:T(8,128)(2,1)} %bitcast.137, bf16[12,256,256]{2,1,0:T(8,128)(2,1)S(1)} %divide_convert_fusion), kind=kOutput, calls=%fused_computation.51 | convolution fusion | flops 201719808 | bytes 3145728 | tf_op jit(solution)/shard_map/hij,jhd->ihd/dot_general | solution.py:124
  56.7 2.6 %copy.20 = bf16[256,12,128]{2,1,0:T(8,128)(2,1)} copy(bf16[256,12,128]{0,2,1:T(8,128)(2,1)} %fusion.23) | data formatting | bytes 1572864 | tf_op jit(solution)/shard_map/convert_element_type | solution.py:130
  59.3 2.4 %dot_general.27 = bf16[2,2,64,1536]{3,2,1,0:T(8,128)(2,1)} reshape(bf16[256,12,128]{2,1,0:T(8,128)(2,1)} %copy.20) | data formatting | bytes 1572864 | tf_op jit(solution)/shard_map/dot_general | solution.py:135
  61.7 8.3 %fusion.6 = f32[2,2,64,3072]{3,2,1,0:T(8,128)} fusion(bf16[2,2,64,1536]{3,2,1,0:T(8,128)(2,1)} %dot_general.27, bf16[1536,6144]{1,0:T(8,128)(2,1)} %bitcast.144), kind=kOutput, calls=%fused_computation.8 | convolution fusion | flops 2415919104 | bytes 13369344 | tf_op jit(solution)/shard_map/dot_general | solution.py:135
  70.0 8.1 %fusion.5 = f32[2,2,64,3072]{3,2,1,0:T(8,128)} fusion(bf16[2,2,64,1536]{3,2,1,0:T(8,128)(2,1)S(1)} %copy-done.11, bf16[1536,6144]{1,0:T(8,128)(2,1)} %bitcast.145), kind=kOutput, calls=%fused_computation.6 | convolution fusion | flops 2415919104 | bytes 13369344 | tf_op jit(solution)/shard_map/dot_general | solution.py:135
  78.2 1.7 %select_bitcast_fusion.1 = (bf16[2,1,64,6144]{3,2,0,1:T(8,128)(2,1)S(1)}, bf16[2,1,64,6144]{3,2,0,1:T(8,128)(2,1)S(1)}) fusion(bf16[2,64,6144]{2,1,0:T(8,128)(2,1)} %collective-permute-done.9, pred[]{:T(512)S(6)} %eq.18, bf16[1,64,6144]{2,1,0:T(8,128)(2,1)S(1)} %copy-done.4, bf16[1,64,6144]{2,1,0:T(8,128)(2,1)S(1)} %get-tuple-element.13), kind=kLoop, calls=%fused_computation.42 | loop fusion | flops 2359296 | bytes 6291457 | tf_op jit(solution)/shard_map/stack | solution.py:40
  80.5 9.1 %convolution_convert_fusion = bf16[256,1536]{1,0:T(8,128)(2,1)S(1)} fusion(bf16[256,6144]{1,0:T(8,128)(2,1)S(1)} %bitcast.135, bf16[1,1536,6144]{2,1,0:T(8,128)(2,1)} %param.15), kind=kOutput, calls=%fused_computation.17 | convolution fusion | flops 4832231424 | bytes 22806528 | tf_op jit(solution)/shard_map/dot_general | solution.py:97
  89.6 1.2 copy.23
  90.8 1.5 fusion.24
  92.3 1.0 copy.24
  93.3 0.5 dot_general.32
  93.9 9.4 %fusion.1 = f32[2,2,64,6144]{3,2,1,0:T(8,128)S(1)} fusion(bf16[2,2,64,1536]{3,2,1,0:T(8,128)(2,1)S(1)} %dot_general.32, bf16[1,6144,1536]{2,1,0:T(8,128)(2,1)} %param.14), kind=kOutput, calls=%fused_computation.1 | convolution fusion | flops 4831838208 | bytes 25952256 | tf_op jit(solution)/shard_map/dot_general | solution.py:108
  103.7 0.6 collective-permute-start.10
  104.2 1.0 copy-done.9
  106.0 1.6 collective-permute-start.3
  107.6 1.6 collective-permute-done.5
  109.3 1.6 collective-permute-start.6
  111.4 0.6 collective-permute-start.11
  112.0 6.1 %collective-permute-done.3 = bf16[64,3072]{1,0:T(8,128)(2,1)S(1)} collective-permute-done((bf16[64,3072]{1,0:T(8,128)(2,1)S(1)}, bf16[64,3072]{1,0:T(8,128)(2,1)S(1)}, u32[]{:S(2)}, u32[]{:S(2)}) %collective-permute-start.3) | collective-permute-done | bytes 393248 | tf_op jit(solution)/shard_map/ppermute | solution.py:14
  118.2 1.6 collective-permute-start.4
  119.8 6.7 %collective-permute-done.6 = bf16[64,3072]{1,0:T(8,128)(2,1)S(1)} collective-permute-done((bf16[64,3072]{1,0:T(8,128)(2,1)S(1)}, bf16[64,3072]{1,0:T(8,128)(2,1)S(1)}, u32[]{:S(2)}, u32[]{:S(2)}) %collective-permute-start.6) | collective-permute-done | bytes 393248 | tf_op jit(solution)/shard_map/ppermute | solution.py:14
  126.6 1.6 collective-permute-start.7
  128.2 14.3 %collective-permute-done.11 = bf16[64,6144]{1,0:T(8,128)(2,1)S(1)} collective-permute-done((bf16[64,6144]{1,0:T(8,128)(2,1)S(1)}, bf16[64,6144]{1,0:T(8,128)(2,1)S(1)}, u32[]{:S(2)}, u32[]{:S(2)}) %collective-permute-start.11) | collective-permute-done | bytes 786464 | tf_op jit(solution)/shard_map/ppermute | solution.py:14
  142.6 1.7 %fusion.15 = (f32[64]{0:T(128)S(1)}, f32[64]{0:T(128)S(1)}) fusion(bf16[64,6144]{1,0:T(8,128)(2,1)} %collective-permute-done.12, bf16[64,6144]{1,0:T(8,128)(2,1)S(1)} %collective-permute-done.11, f32[2,64,6144]{2,1,0:T(8,128)S(1)} %bitcast_add_fusion, s32[]{:T(128)S(6)} %select_n.94, f32[6144]{0:T(1024)S(1)} %bitcast.142), kind=kLoop, calls=%fused_computation.28 | loop fusion | flops 3145600 | bytes 3170820 | tf_op jit(solution)/shard_map/reduce_sum | solution.py:114
  144.3 1.9 %fusion.18 = bf16[64,6144]{1,0:T(8,128)(2,1)S(1)} fusion(bf16[64,6144]{1,0:T(8,128)(2,1)} %collective-permute-done.12, bf16[64,6144]{1,0:T(8,128)(2,1)S(1)} %collective-permute-done.11, f32[2,64,6144]{2,1,0:T(8,128)S(1)} %bitcast_add_fusion, s32[]{:T(128)S(6)} %select_n.94, f32[64]{0:T(128)S(1)} %get-tuple-element.20, f32[64]{0:T(128)S(1)} %get-tuple-element.7, ...), kind=kLoop, calls=%fused_computation.31 | loop fusion | flops 4325376 | bytes 4743940 | tf_op jit(solution)/shard_map/convert_element_type | solution.py:120
  146.2 0.6 collective-permute-start.13
  146.8 2.5 %broadcast_select_fusion = bf16[1,2,64,6144]{3,2,1,0:T(8,128)(2,1)} fusion(bf16[1,2,64,6144]{3,2,1,0:T(8,128)(2,1)S(1)} %copy-done.6, pred[2]{0:T(512)(128)(4,1)S(1)} %iota_compare_fusion.1, bf16[64,6144]{1,0:T(8,128)(2,1)} %collective-permute-done.14), kind=kLoop, calls=%fused_computation.47 | loop fusion | flops 786432 | bytes 3932162 | tf_op jit(solution)/shard_map/jit(_where)/select_n | solution.py:144
  149.3 0.9 maximum_bitcast_fusion
  150.2 15.7 %collective-permute-done.13 = bf16[64,6144]{1,0:T(8,128)(2,1)S(1)} collective-permute-done((bf16[64,6144]{1,0:T(8,128)(2,1)S(1)}, bf16[64,6144]{1,0:T(8,128)(2,1)S(1)}, u32[]{:S(2)}, u32[]{:S(2)}) %collective-permute-start.13) | collective-permute-done | bytes 786464 | tf_op jit(solution)/shard_map/ppermute | solution.py:19
  165.9 0.9 copy.32
  (72 shorter events, 4.9 us)
Async XLA Ops:
  0.6 5.1 %copy-start = (s32[8,2]{0,1:T(2,128)S(1)}, s32[8,2]{0,1:T(2,128)}, u32[]{:S(2)}) copy-start(s32[8,2]{0,1:T(2,128)} %param.11) | copy-start | bytes 196
  0.6 7.6 %copy-start.5 = (bf16[1,2,64,6144]{3,2,1,0:T(8,128)(2,1)S(1)}, bf16[1,2,64,6144]{3,2,1,0:T(8,128)(2,1)}, u32[]{:S(2)}) copy-start(bf16[1,2,64,6144]{3,2,1,0:T(8,128)(2,1)} %param.10) | copy-start | bytes 4718596
  0.7 38.4 %collective-permute-start.8 = (bf16[64,6144]{1,0:T(8,128)(2,1)}, bf16[64,6144]{1,0:T(8,128)(2,1)}, u32[]{:S(2)}, u32[]{:S(2)}) collective-permute-start(bf16[64,6144]{1,0:T(8,128)(2,1)} %bitcast.138), channel_id=1, source_target_pairs={{0,2},{1,3},{2,0},{3,1},{4,6},{5,7},{6,4},{7,5},{8,10},{9,11},{10,... | collective-permute-start | bytes 2359304 | tf_op jit(solution)/shard_map/ppermute | solution.py:14
  3.6 7.1 %copy-start.2 = (bf16[1,64,6144]{2,1,0:T(8,128)(2,1)S(1)}, bf16[1,64,6144]{2,1,0:T(8,128)(2,1)}, u32[]{:S(2)}) copy-start(bf16[1,64,6144]{2,1,0:T(8,128)(2,1)} %param.8) | copy-start | bytes 2359300
  5.1 32.1 %collective-permute-start = (bf16[64,6144]{1,0:T(8,128)(2,1)S(1)}, bf16[64,6144]{1,0:T(8,128)(2,1)}, u32[]{:S(2)}, u32[]{:S(2)}) collective-permute-start(bf16[64,6144]{1,0:T(8,128)(2,1)S(1)} %fusion.13), channel_id=1, source_target_pairs={{0,2},{1,3},{2,0},{3,1},{4,6},{5,7},{6,4},{7,5},{8,10},{9,11},{10,... | collective-permute-start | bytes 2359304 | tf_op jit(solution)/shard_map/ppermute | solution.py:14
  9.2 95.0 %collective-permute-start.12 = (bf16[64,6144]{1,0:T(8,128)(2,1)}, bf16[64,6144]{1,0:T(8,128)(2,1)}, u32[]{:S(2)}, u32[]{:S(2)}) collective-permute-start(bf16[64,6144]{1,0:T(8,128)(2,1)} %dynamic-slice_bitcast_fusion), channel_id=1, source_target_pairs={{28,0},{24,4},{20,8},{16,12},{12,16},{8,20},{4,24},{0,28},{29,1},{... | collective-permute-start | bytes 2359304 | tf_op jit(solution)/shard_map/ppermute | solution.py:24
  10.8 136.0 %collective-permute-start.14 = (bf16[64,6144]{1,0:T(8,128)(2,1)S(1)}, bf16[64,6144]{1,0:T(8,128)(2,1)}, u32[]{:S(2)}, u32[]{:S(2)}) collective-permute-start(bf16[64,6144]{1,0:T(8,128)(2,1)S(1)} %bitcast.131), channel_id=1, source_target_pairs={{28,0},{24,4},{20,8},{16,12},{12,16},{8,20},{4,24},{0,28},{29,1},{... | collective-permute-start | bytes 2359304 | tf_op jit(solution)/shard_map/ppermute | solution.py:24
  12.9 30.9 %slice-start = ((s8[18874368]{0:T(1024)(128)(4,1)}), s8[4194304]{0:T(1024)(128)(4,1)S(1)}, s32[]{:S(2)}) async-start(s8[18874368]{0:T(1024)(128)(4,1)} %bitcast.146), calls=%async_computation | async-start | bytes 8388608
  17.4 19.8 %copy-start.12 = (f32[1,6144]{1,0:T(1,128)S(1)}, f32[1,6144]{1,0:T(1,128)}, u32[]{:S(2)}) copy-start(f32[1,6144]{1,0:T(1,128)} %param.12) | copy-start | bytes 73732
  17.4 26.4 %slice-start.1 = ((s8[18874368]{0:T(1024)(128)(4,1)}), s8[4194304]{0:T(1024)(128)(4,1)S(1)}, s32[]{:S(2)}) async-start(s8[18874368]{0:T(1024)(128)(4,1)} %bitcast.146), calls=%async_computation.1 | async-start | bytes 8388608
  38.8 1.1 copy-start.7
  38.8 5.0 %slice-start.2 = ((s8[18874368]{0:T(1024)(128)(4,1)}), s8[4194304]{0:T(1024)(128)(4,1)S(1)}, s32[]{:S(2)}) async-start(s8[18874368]{0:T(1024)(128)(4,1)} %bitcast.146), calls=%async_computation.2 | async-start | bytes 8388608
  39.0 4.0 %collective-permute-start.1 = (bf16[2,64,6144]{2,1,0:T(8,128)(2,1)S(1)}, bf16[2,64,6144]{2,1,0:T(8,128)(2,1)S(1)}, u32[]{:S(2)}, u32[]{:S(2)}) collective-permute-start(bf16[2,64,6144]{2,1,0:T(8,128)(2,1)S(1)} %pad_maximum_fusion.2), channel_id=1, source_target_pairs={{0,1},{1,0},{2,3},{3,2},{4,5},{5,4},{6,7},{7,6},{8,9},{9,8},{10,11... | collective-permute-start | bytes 4718600 | tf_op jit(solution)/shard_map/ppermute | solution.py:14
  41.6 1.4 copy-start.3
  43.0 2.2 %slice-start.3 = ((s8[18874368]{0:T(1024)(128)(4,1)}), s8[4194304]{0:T(1024)(128)(4,1)S(1)}, s32[]{:S(2)}) async-start(s8[18874368]{0:T(1024)(128)(4,1)} %bitcast.146), calls=%async_computation.3 | async-start | bytes 8388608
  43.0 35.2 %collective-permute-start.9 = (bf16[2,64,6144]{2,1,0:T(8,128)(2,1)}, bf16[2,64,6144]{2,1,0:T(8,128)(2,1)}, u32[]{:S(2)}, u32[]{:S(2)}) collective-permute-start(bf16[2,64,6144]{2,1,0:T(8,128)(2,1)} %pad_maximum_fusion.3), channel_id=1, source_target_pairs={{0,1},{1,0},{2,3},{3,2},{4,5},{5,4},{6,7},{7,6},{8,9},{9,8},{10,11... | collective-permute-start | bytes 4718600 | tf_op jit(solution)/shard_map/ppermute | solution.py:14
  43.2 2.7 %slice-start.4 = ((s8[18874368]{0:T(1024)(128)(4,1)}), s8[2097152]{0:T(1024)(128)(4,1)S(1)}, s32[]{:S(2)}) async-start(s8[18874368]{0:T(1024)(128)(4,1)} %bitcast.146), calls=%async_computation.4 | async-start | bytes 4194304
  61.7 8.3 %copy-start.11 = (bf16[2,2,64,1536]{3,2,1,0:T(8,128)(2,1)S(1)}, bf16[2,2,64,1536]{3,2,1,0:T(8,128)(2,1)}, u32[]{:S(2)}) copy-start(bf16[2,2,64,1536]{3,2,1,0:T(8,128)(2,1)} %dot_general.27) | copy-start | bytes 2359300
  70.0 8.2 %copy-start.4 = (bf16[1,64,6144]{2,1,0:T(8,128)(2,1)S(1)}, bf16[1,64,6144]{2,1,0:T(8,128)(2,1)}, u32[]{:S(2)}) copy-start(bf16[1,64,6144]{2,1,0:T(8,128)(2,1)} %copy-done.3) | copy-start | bytes 2359300
  93.9 9.4 %copy-start.10 = (f32[2,2,64,3072]{3,2,1,0:T(8,128)S(1)}, f32[2,2,64,3072]{3,2,1,0:T(8,128)}, u32[]{:S(2)}) copy-start(f32[2,2,64,3072]{3,2,1,0:T(8,128)} %fusion.6) | copy-start | bytes 9437188
  103.4 1.9 %copy-start.9 = (f32[2,2,64,3072]{3,2,1,0:T(8,128)S(1)}, f32[2,2,64,3072]{3,2,1,0:T(8,128)}, u32[]{:S(2)}) copy-start(f32[2,2,64,3072]{3,2,1,0:T(8,128)} %fusion.5) | copy-start | bytes 9437188
  103.4 2.4 %collective-permute-start.2 = (bf16[2,64,3072]{2,1,0:T(8,128)(2,1)S(1)}, bf16[2,64,3072]{2,1,0:T(8,128)(2,1)S(1)}, u32[]{:S(2)}, u32[]{:S(2)}) collective-permute-start(bf16[2,64,3072]{2,1,0:T(8,128)(2,1)S(1)} %fusion.25), channel_id=1, source_target_pairs={{0,1},{1,0},{2,3},{3,2},{4,5},{5,4},{6,7},{7,6},{8,9},{9,8},{10,11... | collective-permute-start | bytes 2359304 | tf_op jit(solution)/shard_map/ppermute | solution.py:14
  103.7 7.2 %collective-permute-start.10 = (bf16[2,64,6144]{2,1,0:T(8,128)(2,1)S(1)}, bf16[2,64,6144]{2,1,0:T(8,128)(2,1)S(1)}, u32[]{:S(2)}, u32[]{:S(2)}) collective-permute-start(bf16[2,64,6144]{2,1,0:T(8,128)(2,1)S(1)} %fusion.19), channel_id=1, source_target_pairs={{0,1},{1,0},{2,3},{3,2},{4,5},{5,4},{6,7},{7,6},{8,9},{9,8},{10,11... | collective-permute-start | bytes 4718600 | tf_op jit(solution)/shard_map/ppermute | solution.py:14
  105.4 3.7 %collective-permute-start.5 = (bf16[2,64,3072]{2,1,0:T(8,128)(2,1)S(1)}, bf16[2,64,3072]{2,1,0:T(8,128)(2,1)S(1)}, u32[]{:S(2)}, u32[]{:S(2)}) collective-permute-start(bf16[2,64,3072]{2,1,0:T(8,128)(2,1)S(1)} %fusion.27), channel_id=1, source_target_pairs={{0,1},{1,0},{2,3},{3,2},{4,5},{5,4},{6,7},{7,6},{8,9},{9,8},{10,11... | collective-permute-start | bytes 2359304 | tf_op jit(solution)/shard_map/ppermute | solution.py:14
  106.0 12.1 %collective-permute-start.3 = (bf16[64,3072]{1,0:T(8,128)(2,1)S(1)}, bf16[64,3072]{1,0:T(8,128)(2,1)S(1)}, u32[]{:S(2)}, u32[]{:S(2)}) collective-permute-start(bf16[64,3072]{1,0:T(8,128)(2,1)S(1)} %fusion.32), channel_id=1, source_target_pairs={{0,2},{1,3},{2,0},{3,1},{4,6},{5,7},{6,4},{7,5},{8,10},{9,11},{10,... | collective-permute-start | bytes 1179656 | tf_op jit(solution)/shard_map/ppermute | solution.py:14
  109.3 17.1 %collective-permute-start.6 = (bf16[64,3072]{1,0:T(8,128)(2,1)S(1)}, bf16[64,3072]{1,0:T(8,128)(2,1)S(1)}, u32[]{:S(2)}, u32[]{:S(2)}) collective-permute-start(bf16[64,3072]{1,0:T(8,128)(2,1)S(1)} %fusion.33), channel_id=1, source_target_pairs={{0,2},{1,3},{2,0},{3,1},{4,6},{5,7},{6,4},{7,5},{8,10},{9,11},{10,... | collective-permute-start | bytes 1179656 | tf_op jit(solution)/shard_map/ppermute | solution.py:14
  111.4 31.2 %copy-start.13 = (f32[1,6144]{1,0:T(1,128)S(1)}, f32[1,6144]{1,0:T(1,128)}, u32[]{:S(2)}) copy-start(f32[1,6144]{1,0:T(1,128)} %param.12) | copy-start | bytes 73732
  111.4 31.2 %collective-permute-start.11 = (bf16[64,6144]{1,0:T(8,128)(2,1)S(1)}, bf16[64,6144]{1,0:T(8,128)(2,1)S(1)}, u32[]{:S(2)}, u32[]{:S(2)}) collective-permute-start(bf16[64,6144]{1,0:T(8,128)(2,1)S(1)} %fusion.26), channel_id=1, source_target_pairs={{0,2},{1,3},{2,0},{3,1},{4,6},{5,7},{6,4},{7,5},{8,10},{9,11},{10,... | collective-permute-start | bytes 2359304 | tf_op jit(solution)/shard_map/ppermute | solution.py:14
  118.2 31.1 %collective-permute-start.4 = (bf16[64,3072]{1,0:T(8,128)(2,1)S(1)}, bf16[64,3072]{1,0:T(8,128)(2,1)S(1)}, u32[]{:S(2)}, u32[]{:S(2)}) collective-permute-start(bf16[64,3072]{1,0:T(8,128)(2,1)S(1)} %fusion.31), channel_id=1, source_target_pairs={{28,0},{0,4},{4,8},{8,12},{12,16},{16,20},{20,24},{24,28},{29,1},{... | collective-permute-start | bytes 1179656 | tf_op jit(solution)/shard_map/ppermute | solution.py:19
  126.6 17.7 %copy-start.8 = (bf16[1,64,6144]{2,1,0:T(8,128)(2,1)S(1)}, bf16[1,64,6144]{2,1,0:T(8,128)(2,1)}, u32[]{:S(2)}) copy-start(bf16[1,64,6144]{2,1,0:T(8,128)(2,1)} %param.9) | copy-start | bytes 2359300
  126.6 22.6 %collective-permute-start.7 = (bf16[64,3072]{1,0:T(8,128)(2,1)S(1)}, bf16[64,3072]{1,0:T(8,128)(2,1)S(1)}, u32[]{:S(2)}, u32[]{:S(2)}) collective-permute-start(bf16[64,3072]{1,0:T(8,128)(2,1)S(1)} %fusion.29), channel_id=1, source_target_pairs={{28,0},{0,4},{4,8},{8,12},{12,16},{16,20},{20,24},{24,28},{29,1},{... | collective-permute-start | bytes 1179656 | tf_op jit(solution)/shard_map/ppermute | solution.py:19
  144.3 2.5 %copy-start.6 = (bf16[1,2,64,6144]{3,2,1,0:T(8,128)(2,1)S(1)}, bf16[1,2,64,6144]{3,2,1,0:T(8,128)(2,1)}, u32[]{:S(2)}) copy-start(bf16[1,2,64,6144]{3,2,1,0:T(8,128)(2,1)} %param.10) | copy-start | bytes 4718596
  146.2 19.7 %collective-permute-start.13 = (bf16[64,6144]{1,0:T(8,128)(2,1)S(1)}, bf16[64,6144]{1,0:T(8,128)(2,1)S(1)}, u32[]{:S(2)}, u32[]{:S(2)}) collective-permute-start(bf16[64,6144]{1,0:T(8,128)(2,1)S(1)} %fusion.18), channel_id=1, source_target_pairs={{4,0},{8,4},{12,8},{16,12},{20,16},{24,20},{28,24},{0,28},{5,1},{9... | collective-permute-start | bytes 2359304 | tf_op jit(solution)/shard_map/ppermute | solution.py:19
  146.8 20.1 %copy-start.1 = (s32[8,2]{0,1:T(2,128)S(1)}, s32[8,2]{0,1:T(2,128)}, u32[]{:S(2)}) copy-start(s32[8,2]{0,1:T(2,128)} %param.11) | copy-start | bytes 196

commit v2 on v1

--- a/solution.py
+++ b/solution.py
@@ -1,6 +1,10 @@
+import functools
+
 import jax
 import jax.numpy as jnp
 from jax import lax
+from jax.experimental import pallas as pl
+from jax.experimental.pallas import tpu as pltpu
 from jax.sharding import PartitionSpec as P
 
 
@@ -28,18 +32,11 @@
     return lax.axis_size("tp").bit_length() - 1
 
 
-def own_bit(bit):
-    return lax.axis_index("tp") >> bit & 1
-
-
 def gather_rows(block):
     blocks = block
     for done, bit in enumerate(reversed(range(tp_bits()))):
         other = from_partner(blocks, bit)
-        first = own_bit(bit) == 0
-        blocks = jnp.stack(
-            [jnp.where(first, blocks, other), jnp.where(first, other, blocks)], axis=done
-        )
+        blocks = jnp.stack([blocks, other], axis=done)
     return blocks.reshape(-1, block.shape[1])
 
 
@@ -48,8 +45,8 @@
     part = partial.reshape((2,) * bits + (-1, partial.shape[1]))
     for bit in range(bits):
         at = bits - 1 - bit
-        keep = lax.dynamic_index_in_dim(part, own_bit(bit), at, keepdims=False)
-        give = lax.dynamic_index_in_dim(part, 1 - own_bit(bit), at, keepdims=False)
+        keep = lax.index_in_dim(part, 0, at, keepdims=False)
+        give = lax.index_in_dim(part, 1, at, keepdims=False)
         got = from_partner(give.astype(jnp.bfloat16), bit)
         part = keep.astype(jnp.float32) + got.astype(jnp.float32)
     return part
@@ -70,6 +67,53 @@
     return (expo / jnp.sum(expo, axis=-1, keepdims=True)).astype(jnp.bfloat16)
 
 
+def mix_kernel(blocks, over_queries, probs_ref, x_ref, out_ref, ordered, mixed):
+    me = lax.axis_index("tp")
+    rows = x_ref.shape[0] // blocks
+    heads = probs_ref.shape[0]
+    head = x_ref.shape[1] // heads
+    for j in range(blocks):
+        at = pl.ds(pl.multiple_of((me ^ j) * rows, rows), rows)
+        ordered[at, :] = x_ref[j * rows : (j + 1) * rows, :]
+    for h in range(heads):
+        columns = slice(h * head, (h + 1) * head)
+        mixed[:, columns] = lax.dot_general(
+            probs_ref[h],
+            ordered[:, columns],
+            (((0 if over_queries else 1,), (0,)), ((), ())),
+            preferred_element_type=jnp.float32,
+        )
+    for j in range(blocks):
+        at = pl.ds(pl.multiple_of((me ^ j) * rows, rows), rows)
+        out_ref[j * rows : (j + 1) * rows, :] = mixed[at, :].astype(out_ref.dtype)
+
+
+def mix_tokens(probs, x, over_queries):
+    heads, length, _ = probs.shape
+    group = max(g for g in range(1, 5) if heads % g == 0)
+    span = x.shape[1] // heads * group
+    return pl.pallas_call(
+        functools.partial(mix_kernel, lax.axis_size("tp"), over_queries),
+        grid=(heads // group,),
+        in_specs=[
+            pl.BlockSpec((group, length, length), lambda i: (i, 0, 0)),
+            pl.BlockSpec((length, span), lambda i: (0, i)),
+        ],
+        out_specs=pl.BlockSpec((length, span), lambda i: (0, i)),
+        out_shape=jax.ShapeDtypeStruct(x.shape, jnp.bfloat16),
+        scratch_shapes=[
+            pltpu.VMEM((length, span), jnp.bfloat16),
+            pltpu.VMEM((length, span), jnp.float32),
+        ],
+        compiler_params=pltpu.CompilerParams(vmem_limit_bytes=8 << 20),
+        cost_estimate=pl.CostEstimate(
+            flops=2 * length * length * x.shape[1],
+            bytes_accessed=2 * probs.size + 4 * x.size,
+            transcendentals=0,
+        ),
+    )(probs, x)
+
+
 def body(incoming, grad_in, held, roster, norm_gain, r_scores, value_weight, out_weight):
     tokens_here = incoming[0]
     grad_here = grad_in[0]
@@ -77,8 +121,6 @@
     gain = norm_gain[0]
     w_value = value_weight[0]
     w_out = out_weight[0]
-    heads_here = r_scores.shape[1]
-    seq_len = r_scores.shape[2]
     width = tokens_here.shape[1]
     sections = lax.axis_size("section")
     mirror = sections - 1 - lax.axis_index("section")
@@ -97,13 +139,7 @@
     grad_context = lax.dot_general(
         all_grads, w_out, (((1,), (1,)), ((), ())), preferred_element_type=jnp.float32
     ).astype(jnp.bfloat16)
-    grad_values = jnp.einsum(
-        "hij,ihd->jhd",
-        attn_probs,
-        grad_context.reshape(seq_len, heads_here, -1),
-        preferred_element_type=jnp.float32,
-    )
-    grad_values = grad_values.astype(jnp.bfloat16).reshape(seq_len, -1)
+    grad_values = mix_tokens(attn_probs, grad_context, True)
     grad_normed = scatter_rows(
         lax.dot_general(
             grad_values, w_value, (((1,), (1,)), ((), ())), preferred_element_type=jnp.float32
@@ -121,13 +157,7 @@
 
     values = jnp.dot(all_normed, w_value, preferred_element_type=jnp.float32)
     values = values.astype(jnp.bfloat16)
-    context = jnp.einsum(
-        "hij,jhd->ihd",
-        attn_probs,
-        values.reshape(seq_len, heads_here, -1),
-        preferred_element_type=jnp.float32,
-    )
-    context = context.astype(jnp.bfloat16).reshape(seq_len, -1)
+    context = mix_tokens(attn_probs, values, False)
     passed_on = []
     span = width // CHUNKS
     for k in range(CHUNKS):

time: 170 us -> 152 us (0.89)
  local copies, waits for them, and re-layouts: 17.7 us -> 6.33 us
  other arithmetic: 23.8 us -> 17.6 us
  matrix products: 45 us -> 39 us
  waiting for transfers between devices: 63.9 us -> 67.3 us
  Pallas kernels: 0 us -> 2.53 us
    convert_element_type x4 -> x0, local copies, waits for them, and re-layouts: 7.08 us -> none  [the longest x1 2.61 us: body(): context = context.astype(jnp.bfloat16).reshape(seq_len, -1)]
    another operation x8 -> x4, other arithmetic: 7.28 us -> 2.27 us  [gather_rows(): blocks = jnp.stack([blocks, other], axis=done)]
    dot_general x2, matrix products: 16.4 us -> 11.5 us  [body(): jnp.dot(context, w_out[:, columns], preferred_element_type=jnp.float32)]
    dot_general x2 -> x0, matrix products: 4.16 us -> none  [the longest x1 2.65 us: body(): jnp.einsum('hij,jhd->ihd', attn_probs, values.reshape(seq_len, heads_here...]
    dot_general x1, matrix products: 5.9 us -> 9.29 us  [body(): values = jnp.dot(all_normed, w_value, preferred_element_type=jnp.float32)]
    ppermute x10, waiting for transfers between devices: 48.2 us -> 51.5 us  [from_partner(): lax.ppermute(value, 'tp', [(i, i ^ 1 << bit) for i in range(lax.axis_size...]
    dot_general x2 -> x0, local copies, waits for them, and re-layouts: 2.9 us -> none  [the longest x1 2.37 us: body(): jnp.dot(context, w_out[:, columns], preferred_element_type=jnp.float32)]
    pallas_call x0 -> x2, Pallas kernels: none -> 2.53 us  [mix_tokens(): pl.pallas_call(functools.partial(mix_kernel, lax.axis_size('tp'), over_qu...]
  transfers between devices with their start and end apart: 15 -> 15, of which waited for: 7 -> 5; matrix products, arithmetic and copies ran while one was open for 49% -> 38% of each run, Pallas kernels for 0% -> 2%
where the time goes in v2:
time: 152 us; the launch traced here: 149 us
  waiting for transfers between devices  67.3 us (44%)
  matrix products  39 us (26%)
  other arithmetic  17.6 us (12%)
  starting transfers between devices  13.7 us (9%)
  local copies, waits for them, and re-layouts  6.33 us (4%)
  between operations  2.96 us (2%)
  Pallas kernels  2.53 us (2%)
    ppermute x10, waiting for transfers between devices, from_partner(): lax.ppermute(value, 'tp', [(i, i ^ 1 << bit) for i in range(lax.axis_size...  51.5 us
    ppermute x3, waiting for transfers between devices, from_behind(): lax.ppermute(block, 'section', [((i - distance) % len(devices), i) for i...  15.9 us
    dot_general x2, matrix products, body(): jnp.dot(context, w_out[:, columns], preferred_element_type=jnp.float32)  11.5 us
    dot_general x1, matrix products, body(): values = jnp.dot(all_normed, w_value, preferred_element_type=jnp.float32)  9.29 us
    dot_general x1, matrix products, body(): lax.dot_general(all_grads, w_out, (((1,), (1,)), ((), ())), preferred_ele...  9.1 us
    dot_general x1, matrix products, body(): lax.dot_general(grad_values, w_value, (((1,), (1,)), ((), ())), preferred...  9.08 us
    ppermute x10, starting transfers between devices, from_partner(): lax.ppermute(value, 'tp', [(i, i ^ 1 << bit) for i in range(lax.axis_size...  6.97 us
    ppermute x3, starting transfers between devices, from_behind(): lax.ppermute(block, 'section', [((i - distance) % len(devices), i) for i...  3.7 us
  transfers between devices with their start and end apart: 15, of which 5 were waited for; matrix products, arithmetic and copies ran while one was open for 38% of the time, Pallas kernels for 2%

profile of v2, /device:TPU:12, one launch (start us, length us, event | category | flops | bytes accessed | tf_op | source)
XLA Modules:
  0.0 149.4 jit_solution(14657764967715957811)
XLA Ops:
  0.7 1.5 %fusion.14 = f32[64]{0:T(128)S(1)} fusion(bf16[1,64,6144]{2,1,0:T(8,128)(2,1)} %param.8), kind=kLoop, calls=%fused_computation.25 | loop fusion | flops 1179584 | bytes 786688 | tf_op jit(solution)/shard_map/reduce_sum | solution.py:56
  2.2 2.4 %fusion.16 = bf16[64,6144]{1,0:T(8,128)(2,1)} fusion(f32[6144]{0:T(1024)} %bitcast.123, f32[64]{0:T(128)S(1)} %add_sqrt_fusion.1, bf16[1,64,6144]{2,1,0:T(8,128)(2,1)} %param.8), kind=kLoop, calls=%fused_computation.27 | loop fusion | flops 1572864 | bytes 1597696 | tf_op jit(solution)/shard_map/convert_element_type | solution.py:130
  4.6 1.5 collective-permute-start
  6.2 0.5 fusion.45
  8.7 1.6 %collective-permute-start.12 = (bf16[64,6144]{1,0:T(8,128)(2,1)S(1)}, bf16[64,6144]{1,0:T(8,128)(2,1)S(1)}, u32[]{:S(2)}, u32[]{:S(2)}) collective-permute-start(bf16[64,6144]{1,0:T(8,128)(2,1)S(1)} %dynamic-slice_bitcast_fusion), channel_id=1, source_target_pairs={{28,0},{24,4},{20,8},{16,12},{12,16},{8,20},{4,24},{0,28},{29,1},{... | collective-permute-start | bytes 2359304 | tf_op jit(solution)/shard_map/ppermute | solution.py:28
  10.3 0.5 collective-permute-start.8
  10.9 1.4 collective-permute-start.14
  12.3 0.3 multiply_convert_fusion
  12.6 12.8 %collective-permute-done = bf16[64,6144]{1,0:T(8,128)(2,1)} collective-permute-done((bf16[64,6144]{1,0:T(8,128)(2,1)}, bf16[64,6144]{1,0:T(8,128)(2,1)}, u32[]{:S(2)}, u32[]{:S(2)}) %collective-permute-start) | collective-permute-done | bytes 786464 | tf_op jit(solution)/shard_map/ppermute | solution.py:18
  25.3 1.5 fusion.44
  26.9 0.7 iota_compare_fusion.1
  27.6 2.0 %fusion.46 = (f32[12,256]{1,0:T(8,128)S(1)}, f32[12,256,256]{2,1,0:T(8,128)S(1)}) fusion(f32[1,12,256,256]{3,2,1,0:T(8,128)S(1)} %copy-done.13, pred[256,256]{1,0:T(8,128)(4,1)S(1)} %iota_compare_fusion), kind=kOutput, calls=%fused_computation.79 | output fusion | flops 3932415 | bytes 6369280 | tf_op jit(solution)/shard_map/sub | solution.py:66
  29.6 0.5 divide_convert_fusion.probs_ref
  30.1 10.9 %collective-permute-done.8 = bf16[64,6144]{1,0:T(8,128)(2,1)S(1)} collective-permute-done((bf16[64,6144]{1,0:T(8,128)(2,1)S(1)}, bf16[64,6144]{1,0:T(8,128)(2,1)S(1)}, u32[]{:S(2)}, u32[]{:S(2)}) %collective-permute-start.8) | collective-permute-done | bytes 786464 | tf_op jit(solution)/shard_map/ppermute | solution.py:18
  41.0 0.2 fusion.43
  41.3 0.3 pad_maximum_fusion
  41.6 0.3 copy.16
  41.9 9.3 %fusion.11.x_ref = bf16[256,1536]{1,0:T(8,128)(2,1)S(1)} fusion(bf16[256,6144]{1,0:T(8,128)(2,1)S(1)} %bitcast.112, bf16[1,6144,1536]{2,1,0:T(8,128)(2,1)} %param.14), kind=kOutput, calls=%fused_computation.19 | convolution fusion | flops 4832231424 | bytes 22806528 | tf_op jit(solution)/shard_map/dot_general | solution.py:158
  51.2 1.2 shard_map.103
  52.4 5.2 %fusion.5 = f32[256,3072]{1,0:T(8,128)S(1)} fusion(bf16[256,1536]{1,0:T(8,128)(2,1)S(1)} %shard_map.103, bf16[1536,6144]{1,0:T(8,128)(2,1)} %bitcast.127), kind=kOutput, calls=%fused_computation.5 | convolution fusion | flops 2415919104 | bytes 13369344 | tf_op jit(solution)/shard_map/dot_general | solution.py:165
  57.6 6.3 %fusion.7 = f32[256,3072]{1,0:T(8,128)S(1)} fusion(bf16[256,1536]{1,0:T(8,128)(2,1)S(1)} %shard_map.103, bf16[1536,6144]{1,0:T(8,128)(2,1)} %bitcast.128), kind=kOutput, calls=%fused_computation.7 | convolution fusion | flops 2415919104 | bytes 13369344 | tf_op jit(solution)/shard_map/dot_general | solution.py:165
  64.0 1.1 fusion.31
  65.1 0.5 collective-permute-start.5
  65.6 1.0 fusion.30
  66.6 0.3 pad_maximum_fusion.1
  66.9 0.6 copy-done.5
  67.7 9.1 %convolution_convert_fusion.x_ref = bf16[256,1536]{1,0:T(8,128)(2,1)S(1)} fusion(bf16[256,6144]{1,0:T(8,128)(2,1)S(1)} %bitcast.113, bf16[1,1536,6144]{2,1,0:T(8,128)(2,1)} %param.15), kind=kOutput, calls=%fused_computation.18 | convolution fusion | flops 4832231424 | bytes 22806528 | tf_op jit(solution)/shard_map/dot_general | solution.py:139
  76.8 1.3 shard_map.104
  78.2 9.1 %fusion.1 = f32[2,2,64,6144]{3,2,1,0:T(8,128)S(1)} fusion(bf16[2,2,64,1536]{3,2,1,0:T(8,128)(2,1)S(1)} %bitcast.108, bf16[1,6144,1536]{2,1,0:T(8,128)(2,1)} %param.14), kind=kOutput, calls=%fused_computation.1 | convolution fusion | flops 4831838208 | bytes 25952256 | tf_op jit(solution)/shard_map/dot_general | solution.py:144
  87.5 0.5 collective-permute-start.10
  88.0 1.2 copy-done.10
  89.1 1.3 fusion.23
  90.5 1.6 %collective-permute-start.6 = (bf16[64,3072]{1,0:T(8,128)(2,1)S(1)}, bf16[64,3072]{1,0:T(8,128)(2,1)S(1)}, u32[]{:S(2)}, u32[]{:S(2)}) collective-permute-start(bf16[64,3072]{1,0:T(8,128)(2,1)S(1)} %fusion.39), channel_id=1, source_target_pairs={{0,2},{1,3},{2,0},{3,1},{4,6},{5,7},{6,4},{7,5},{8,10},{9,11},{10,... | collective-permute-start | bytes 1179656 | tf_op jit(solution)/shard_map/ppermute | solution.py:18
  92.1 1.3 fusion.24
  93.4 0.6 collective-permute-start.3
  94.0 0.4 fusion.9
  94.5 1.6 %collective-permute-start.11 = (bf16[64,6144]{1,0:T(8,128)(2,1)S(1)}, bf16[64,6144]{1,0:T(8,128)(2,1)S(1)}, u32[]{:S(2)}, u32[]{:S(2)}) collective-permute-start(bf16[64,6144]{1,0:T(8,128)(2,1)S(1)} %fusion.29), channel_id=1, source_target_pairs={{0,2},{1,3},{2,0},{3,1},{4,6},{5,7},{6,4},{7,5},{8,10},{9,11},{10,... | collective-permute-start | bytes 2359304 | tf_op jit(solution)/shard_map/ppermute | solution.py:18
  96.1 14.9 %collective-permute-done.3 = bf16[64,3072]{1,0:T(8,128)(2,1)S(1)} collective-permute-done((bf16[64,3072]{1,0:T(8,128)(2,1)S(1)}, bf16[64,3072]{1,0:T(8,128)(2,1)S(1)}, u32[]{:S(2)}, u32[]{:S(2)}) %collective-permute-start.3) | collective-permute-done | bytes 393248 | tf_op jit(solution)/shard_map/ppermute | solution.py:18
  111.1 1.6 %collective-permute-start.4 = (bf16[64,3072]{1,0:T(8,128)(2,1)S(1)}, bf16[64,3072]{1,0:T(8,128)(2,1)S(1)}, u32[]{:S(2)}, u32[]{:S(2)}) collective-permute-start(bf16[64,3072]{1,0:T(8,128)(2,1)S(1)} %fusion.37), channel_id=1, source_target_pairs={{28,0},{0,4},{4,8},{8,12},{12,16},{16,20},{20,24},{24,28},{29,1},{... | collective-permute-start | bytes 1179656 | tf_op jit(solution)/shard_map/ppermute | solution.py:23
  112.8 1.6 %collective-permute-start.7 = (bf16[64,3072]{1,0:T(8,128)(2,1)S(1)}, bf16[64,3072]{1,0:T(8,128)(2,1)S(1)}, u32[]{:S(2)}, u32[]{:S(2)}) collective-permute-start(bf16[64,3072]{1,0:T(8,128)(2,1)S(1)} %fusion.34), channel_id=1, source_target_pairs={{28,0},{0,4},{4,8},{8,12},{12,16},{16,20},{20,24},{24,28},{29,1},{... | collective-permute-start | bytes 1179656 | tf_op jit(solution)/shard_map/ppermute | solution.py:23
  114.4 12.9 %collective-permute-done.11 = bf16[64,6144]{1,0:T(8,128)(2,1)S(1)} collective-permute-done((bf16[64,6144]{1,0:T(8,128)(2,1)S(1)}, bf16[64,6144]{1,0:T(8,128)(2,1)S(1)}, u32[]{:S(2)}, u32[]{:S(2)}) %collective-permute-start.11) | collective-permute-done | bytes 786464 | tf_op jit(solution)/shard_map/ppermute | solution.py:18
  127.3 0.6 fusion.18
  127.9 0.6 fusion.21
  128.5 0.6 collective-permute-start.13
  129.1 2.6 %broadcast_select_fusion = bf16[1,2,64,6144]{3,2,1,0:T(8,128)(2,1)} fusion(bf16[1,2,64,6144]{3,2,1,0:T(8,128)(2,1)S(1)} %copy-done.3, pred[2]{0:T(512)(128)(4,1)S(1)} %iota_compare_fusion.1, bf16[64,6144]{1,0:T(8,128)(2,1)} %collective-permute-done.14), kind=kLoop, calls=%fused_computation.48 | loop fusion | flops 786432 | bytes 3932162 | tf_op jit(solution)/shard_map/jit(_where)/select_n | solution.py:174
  131.7 0.9 maximum_bitcast_fusion
  132.6 15.9 %collective-permute-done.13 = bf16[64,6144]{1,0:T(8,128)(2,1)S(1)} collective-permute-done((bf16[64,6144]{1,0:T(8,128)(2,1)S(1)}, bf16[64,6144]{1,0:T(8,128)(2,1)S(1)}, u32[]{:S(2)}, u32[]{:S(2)}) %collective-permute-start.13) | collective-permute-done | bytes 786464 | tf_op jit(solution)/shard_map/ppermute | solution.py:23
  148.5 0.9 copy.42
  (52 shorter events, 1.3 us)
Async XLA Ops:
  0.6 5.5 %copy-start = (s32[8,2]{0,1:T(2,128)S(1)}, s32[8,2]{0,1:T(2,128)}, u32[]{:S(2)}) copy-start(s32[8,2]{0,1:T(2,128)} %param.11) | copy-start | bytes 196
  0.6 8.0 %copy-start.3 = (bf16[1,2,64,6144]{3,2,1,0:T(8,128)(2,1)S(1)}, bf16[1,2,64,6144]{3,2,1,0:T(8,128)(2,1)}, u32[]{:S(2)}) copy-start(bf16[1,2,64,6144]{3,2,1,0:T(8,128)(2,1)} %param.10) | copy-start | bytes 4718596
  2.2 8.1 %copy-start.4 = (bf16[1,64,6144]{2,1,0:T(8,128)(2,1)S(1)}, bf16[1,64,6144]{2,1,0:T(8,128)(2,1)}, u32[]{:S(2)}) copy-start(bf16[1,64,6144]{2,1,0:T(8,128)(2,1)} %param.9) | copy-start | bytes 2359300
  2.2 8.7 %copy-start.2 = (bf16[1,64,6144]{2,1,0:T(8,128)(2,1)S(1)}, bf16[1,64,6144]{2,1,0:T(8,128)(2,1)}, u32[]{:S(2)}) copy-start(bf16[1,64,6144]{2,1,0:T(8,128)(2,1)} %param.8) | copy-start | bytes 2359300
  2.2 10.1 %copy-start.11 = (f32[1,6144]{1,0:T(1,128)S(1)}, f32[1,6144]{1,0:T(1,128)}, u32[]{:S(2)}) copy-start(f32[1,6144]{1,0:T(1,128)} %param.12) | copy-start | bytes 73732
  4.6 20.7 %collective-permute-start = (bf16[64,6144]{1,0:T(8,128)(2,1)}, bf16[64,6144]{1,0:T(8,128)(2,1)}, u32[]{:S(2)}, u32[]{:S(2)}) collective-permute-start(bf16[64,6144]{1,0:T(8,128)(2,1)} %fusion.16), channel_id=1, source_target_pairs={{0,2},{1,3},{2,0},{3,1},{4,6},{5,7},{6,4},{7,5},{8,10},{9,11},{10,... | collective-permute-start | bytes 2359304 | tf_op jit(solution)/shard_map/ppermute | solution.py:18
  8.7 57.9 %collective-permute-start.12 = (bf16[64,6144]{1,0:T(8,128)(2,1)S(1)}, bf16[64,6144]{1,0:T(8,128)(2,1)S(1)}, u32[]{:S(2)}, u32[]{:S(2)}) collective-permute-start(bf16[64,6144]{1,0:T(8,128)(2,1)S(1)} %dynamic-slice_bitcast_fusion), channel_id=1, source_target_pairs={{28,0},{24,4},{20,8},{16,12},{12,16},{8,20},{4,24},{0,28},{29,1},{... | collective-permute-start | bytes 2359304 | tf_op jit(solution)/shard_map/ppermute | solution.py:28
  10.3 30.6 %collective-permute-start.8 = (bf16[64,6144]{1,0:T(8,128)(2,1)S(1)}, bf16[64,6144]{1,0:T(8,128)(2,1)S(1)}, u32[]{:S(2)}, u32[]{:S(2)}) collective-permute-start(bf16[64,6144]{1,0:T(8,128)(2,1)S(1)} %bitcast.114), channel_id=1, source_target_pairs={{0,2},{1,3},{2,0},{3,1},{4,6},{5,7},{6,4},{7,5},{8,10},{9,11},{10,... | collective-permute-start | bytes 2359304 | tf_op jit(solution)/shard_map/ppermute | solution.py:18
  10.9 118.2 %collective-permute-start.14 = (bf16[64,6144]{1,0:T(8,128)(2,1)S(1)}, bf16[64,6144]{1,0:T(8,128)(2,1)}, u32[]{:S(2)}, u32[]{:S(2)}) collective-permute-start(bf16[64,6144]{1,0:T(8,128)(2,1)S(1)} %bitcast.109), channel_id=1, source_target_pairs={{28,0},{24,4},{20,8},{16,12},{12,16},{8,20},{4,24},{0,28},{29,1},{... | collective-permute-start | bytes 2359304 | tf_op jit(solution)/shard_map/ppermute | solution.py:28
  25.3 2.3 %copy-start.13 = (f32[1,12,256,256]{3,2,1,0:T(8,128)S(1)}, f32[1,12,256,256]{3,2,1,0:T(8,128)}, u32[]{:S(2)}) copy-start(f32[1,12,256,256]{3,2,1,0:T(8,128)} %param.13) | copy-start | bytes 9437188
  26.8 14.4 %collective-permute-start.1 = (bf16[2,64,6144]{2,1,0:T(8,128)(2,1)S(1)}, bf16[2,64,6144]{2,1,0:T(8,128)(2,1)S(1)}, u32[]{:S(2)}, u32[]{:S(2)}) collective-permute-start(bf16[2,64,6144]{2,1,0:T(8,128)(2,1)S(1)} %get-tuple-element.12), channel_id=1, source_target_pairs={{0,1},{1,0},{2,3},{3,2},{4,5},{5,4},{6,7},{7,6},{8,9},{9,8},{10,11... | collective-permute-start | bytes 4718600 | tf_op jit(solution)/shard_map/ppermute | solution.py:18
  41.2 25.5 %collective-permute-start.9 = (bf16[2,64,6144]{2,1,0:T(8,128)(2,1)S(1)}, bf16[2,64,6144]{2,1,0:T(8,128)(2,1)S(1)}, u32[]{:S(2)}, u32[]{:S(2)}) collective-permute-start(bf16[2,64,6144]{2,1,0:T(8,128)(2,1)S(1)} %get-tuple-element.10), channel_id=1, source_target_pairs={{0,1},{1,0},{2,3},{3,2},{4,5},{5,4},{6,7},{7,6},{8,9},{9,8},{10,11... | collective-permute-start | bytes 4718600 | tf_op jit(solution)/shard_map/ppermute | solution.py:18
  57.6 6.4 %copy-start.9 = (f32[256,3072]{1,0:T(8,128)}, f32[256,3072]{1,0:T(8,128)S(1)}, u32[]{:S(2)}) copy-start(f32[256,3072]{1,0:T(8,128)S(1)} %fusion.5) | copy-start | bytes 9437188
  63.9 2.6 %copy-start.7 = (f32[256,3072]{1,0:T(8,128)}, f32[256,3072]{1,0:T(8,128)S(1)}, u32[]{:S(2)}) copy-start(f32[256,3072]{1,0:T(8,128)S(1)} %fusion.7) | copy-start | bytes 9437188
  65.1 22.9 %collective-permute-start.5 = (bf16[2,64,3072]{2,1,0:T(8,128)(2,1)}, bf16[2,64,3072]{2,1,0:T(8,128)(2,1)}, u32[]{:S(2)}, u32[]{:S(2)}) collective-permute-start(bf16[2,64,3072]{2,1,0:T(8,128)(2,1)} %fusion.31), channel_id=1, source_target_pairs={{0,1},{1,0},{2,3},{3,2},{4,5},{5,4},{6,7},{7,6},{8,9},{9,8},{10,11... | collective-permute-start | bytes 2359304 | tf_op jit(solution)/shard_map/ppermute | solution.py:18
  66.5 25.5 %collective-permute-start.2 = (bf16[2,64,3072]{2,1,0:T(8,128)(2,1)}, bf16[2,64,3072]{2,1,0:T(8,128)(2,1)}, u32[]{:S(2)}, u32[]{:S(2)}) collective-permute-start(bf16[2,64,3072]{2,1,0:T(8,128)(2,1)} %fusion.30), channel_id=1, source_target_pairs={{0,1},{1,0},{2,3},{3,2},{4,5},{5,4},{6,7},{7,6},{8,9},{9,8},{10,11... | collective-permute-start | bytes 2359304 | tf_op jit(solution)/shard_map/ppermute | solution.py:18
  66.6 0.9 copy-start.5
  87.2 1.9 %copy-start.10 = (f32[256,3072]{1,0:T(8,128)S(1)}, f32[256,3072]{1,0:T(8,128)}, u32[]{:S(2)}) copy-start(f32[256,3072]{1,0:T(8,128)} %copy-done.9) | copy-start | bytes 9437188
  87.5 4.6 %copy-start.8 = (f32[256,3072]{1,0:T(8,128)S(1)}, f32[256,3072]{1,0:T(8,128)}, u32[]{:S(2)}) copy-start(f32[256,3072]{1,0:T(8,128)} %copy-done.7) | copy-start | bytes 9437188
  87.5 6.5 %collective-permute-start.10 = (bf16[2,64,6144]{2,1,0:T(8,128)(2,1)S(1)}, bf16[2,64,6144]{2,1,0:T(8,128)(2,1)S(1)}, u32[]{:S(2)}, u32[]{:S(2)}) collective-permute-start(bf16[2,64,6144]{2,1,0:T(8,128)(2,1)S(1)} %fusion.22), channel_id=1, source_target_pairs={{0,1},{1,0},{2,3},{3,2},{4,5},{5,4},{6,7},{7,6},{8,9},{9,8},{10,11... | collective-permute-start | bytes 4718600 | tf_op jit(solution)/shard_map/ppermute | solution.py:18
  90.5 22.2 %collective-permute-start.6 = (bf16[64,3072]{1,0:T(8,128)(2,1)S(1)}, bf16[64,3072]{1,0:T(8,128)(2,1)S(1)}, u32[]{:S(2)}, u32[]{:S(2)}) collective-permute-start(bf16[64,3072]{1,0:T(8,128)(2,1)S(1)} %fusion.39), channel_id=1, source_target_pairs={{0,2},{1,3},{2,0},{3,1},{4,6},{5,7},{6,4},{7,5},{8,10},{9,11},{10,... | collective-permute-start | bytes 1179656 | tf_op jit(solution)/shard_map/ppermute | solution.py:18
  93.4 17.6 %collective-permute-start.3 = (bf16[64,3072]{1,0:T(8,128)(2,1)S(1)}, bf16[64,3072]{1,0:T(8,128)(2,1)S(1)}, u32[]{:S(2)}, u32[]{:S(2)}) collective-permute-start(bf16[64,3072]{1,0:T(8,128)(2,1)S(1)} %fusion.38), channel_id=1, source_target_pairs={{0,2},{1,3},{2,0},{3,1},{4,6},{5,7},{6,4},{7,5},{8,10},{9,11},{10,... | collective-permute-start | bytes 1179656 | tf_op jit(solution)/shard_map/ppermute | solution.py:18
  94.5 32.8 %copy-start.6 = (bf16[64,6144]{1,0:T(8,128)(2,1)S(1)}, bf16[64,6144]{1,0:T(8,128)(2,1)}, u32[]{:S(2)}) copy-start(bf16[64,6144]{1,0:T(8,128)(2,1)} %copy-done.5) | copy-start | bytes 2359300
  94.5 32.8 %copy-start.12 = (f32[1,6144]{1,0:T(1,128)S(1)}, f32[1,6144]{1,0:T(1,128)}, u32[]{:S(2)}) copy-start(f32[1,6144]{1,0:T(1,128)} %param.12) | copy-start | bytes 73732
  94.5 32.8 %collective-permute-start.11 = (bf16[64,6144]{1,0:T(8,128)(2,1)S(1)}, bf16[64,6144]{1,0:T(8,128)(2,1)S(1)}, u32[]{:S(2)}, u32[]{:S(2)}) collective-permute-start(bf16[64,6144]{1,0:T(8,128)(2,1)S(1)} %fusion.29), channel_id=1, source_target_pairs={{0,2},{1,3},{2,0},{3,1},{4,6},{5,7},{6,4},{7,5},{8,10},{9,11},{10,... | collective-permute-start | bytes 2359304 | tf_op jit(solution)/shard_map/ppermute | solution.py:18
  111.1 20.6 %collective-permute-start.4 = (bf16[64,3072]{1,0:T(8,128)(2,1)S(1)}, bf16[64,3072]{1,0:T(8,128)(2,1)S(1)}, u32[]{:S(2)}, u32[]{:S(2)}) collective-permute-start(bf16[64,3072]{1,0:T(8,128)(2,1)S(1)} %fusion.37), channel_id=1, source_target_pairs={{28,0},{0,4},{4,8},{8,12},{12,16},{16,20},{20,24},{24,28},{29,1},{... | collective-permute-start | bytes 1179656 | tf_op jit(solution)/shard_map/ppermute | solution.py:23
  112.8 18.9 %collective-permute-start.7 = (bf16[64,3072]{1,0:T(8,128)(2,1)S(1)}, bf16[64,3072]{1,0:T(8,128)(2,1)S(1)}, u32[]{:S(2)}, u32[]{:S(2)}) collective-permute-start(bf16[64,3072]{1,0:T(8,128)(2,1)S(1)} %fusion.34), channel_id=1, source_target_pairs={{28,0},{0,4},{4,8},{8,12},{12,16},{16,20},{20,24},{24,28},{29,1},{... | collective-permute-start | bytes 1179656 | tf_op jit(solution)/shard_map/ppermute | solution.py:23
  128.5 20.0 %collective-permute-start.13 = (bf16[64,6144]{1,0:T(8,128)(2,1)S(1)}, bf16[64,6144]{1,0:T(8,128)(2,1)S(1)}, u32[]{:S(2)}, u32[]{:S(2)}) collective-permute-start(bf16[64,6144]{1,0:T(8,128)(2,1)S(1)} %fusion.21), channel_id=1, source_target_pairs={{4,0},{8,4},{12,8},{16,12},{20,16},{24,20},{28,24},{0,28},{5,1},{9... | collective-permute-start | bytes 2359304 | tf_op jit(solution)/shard_map/ppermute | solution.py:23
  129.1 20.3 %copy-start.1 = (s32[8,2]{0,1:T(2,128)S(1)}, s32[8,2]{0,1:T(2,128)}, u32[]{:S(2)}) copy-start(s32[8,2]{0,1:T(2,128)} %param.11) | copy-start | bytes 196
